TPU v7x, 32 devices: a whole 2x2x4 slice. The times are simulated.
32 devices in a mesh: member: 4 (over y, x), tile: 8 (over z, core).
Axes of the slice: x: 2, y: 2, z: 4, core: 2. Of those that a mesh axis runs over, the one named last changes fastest.
Arguments:
- northward_speed_field: float32 [16, 16, 64, 256], P('member', None, 'tile'), may hold values from -6 to 6
- level_depth_extent: float32 [16, 16, 64, 256], P('member', None, 'tile'), may hold values from 0.2 to 5
- potential_warmth_anomaly: float32 [16, 16, 64, 256], P('member', None, 'tile'), may hold values from -6 to 6
- ocean_region_label: int32 [64, 256], P('tile'), may hold values from 0 to 9
- zone_for_parallel: int32 [256], replicated, may hold values from 0 to 15, never falling along the last dimension, each value on 1 to 32 neighbouring positions
Outputs:
- mean_psi: float32 [10, 16, 256], P(None, None, ('member', 'tile'))
- mean_heat: float32 [10, 256], P(None, ('member', 'tile'))
- covariance: float32 [16, 16, 16], replicated
Inputs may be any that keep to these rules, and one draw needn't show every extreme that they name: `zone_for_parallel`: never falls along latitude; every band holds 1 to 32 latitudes.
All inputs are finite; a program needn't handle non-finite values.
Results may differ from a plain program's by a relative error of at most 0.00011.
Values sent between devices are 32-bit elements; how exact they have to be, the bound alone decides.
No kernel may reach another device: no remote copies, remote signals or barrier semaphores. Data moves between devices by JAX's collectives and lax.ppermute only.
A program may use at most 128 MiB of HBM per device.

v0:
```python
import math
import jax
import jax.numpy as jnp
from jax import lax
from jax.sharding import PartitionSpec as P

BASINS = 10
NBANDS = 16


def metric_factor(lats):
    index = jnp.arange(lats, dtype=jnp.float32)
    return jnp.cos((-80.0 + 160.0 * (index + 0.5) / lats) * (math.pi / 180.0))


def local(
    northward_speed_field,
    level_depth_extent,
    potential_warmth_anomaly,
    ocean_region_label,
    zone_for_parallel,
):
    greatest_bound_value = lax.Precision.HIGHEST
    members_here, layers, columns, lats = northward_speed_field.shape
    tiles = lax.axis_size("tile")
    groups = lax.axis_size("member")
    owned = lats // (groups * tiles)
    northward_volume_carriage = northward_speed_field * level_depth_extent * metric_factor(lats)
    region_indicator_matrix = (
        ocean_region_label[None, :, :] == jnp.arange(BASINS, dtype=jnp.int32)[:, None, None]
    ).astype(jnp.float32)
    transport = jnp.einsum(
        "mkxl,bxl->mbkl",
        northward_volume_carriage,
        region_indicator_matrix,
        precision=greatest_bound_value,
    ) / math.sqrt(columns * tiles)
    thermal_energy_integral = jnp.einsum(
        "tzux,pux->tpx",
        northward_volume_carriage * potential_warmth_anomaly,
        region_indicator_matrix,
        precision=greatest_bound_value,
    ) / math.sqrt(columns * tiles * layers)
    partial_value = jnp.concatenate(
        [transport.reshape(members_here, BASINS * layers, lats), thermal_energy_integral], axis=1
    )
    regrouped = lax.all_to_all(partial_value, "member", split_axis=2, concat_axis=0, tiled=True)
    summed = lax.psum_scatter(regrouped, "tile", scatter_dimension=2, tiled=True)
    members = summed.shape[0]
    streams = jnp.cumsum(
        summed[:, : BASINS * layers].reshape(members, BASINS, layers, owned), axis=2
    )
    heat_all = summed[:, BASINS * layers :]
    mean_psi = jnp.mean(streams, axis=0)
    mean_heat = jnp.mean(heat_all, axis=0)
    anomaly = (streams - mean_psi).reshape(members, BASINS * layers, owned)
    start = (lax.axis_index("member") * tiles + lax.axis_index("tile")) * owned
    bands_here = lax.dynamic_slice_in_dim(zone_for_parallel, start, owned)
    band_hot = (bands_here[:, None] == jnp.arange(NBANDS, dtype=jnp.int32)[None, :]).astype(
        jnp.float32
    )
    products = jnp.einsum("mfl,nfl->lmn", anomaly, anomaly, precision=greatest_bound_value)
    norm = float((members - 1) * BASINS * layers * (lats // NBANDS))
    local_cov = jnp.einsum("lmn,lc->cmn", products, band_hot, precision=greatest_bound_value) / norm
    covariance = lax.psum(local_cov, ("member", "tile"))
    return (mean_psi, mean_heat, covariance)


def solution(mesh):
    in_specs = (
        P("member", None, "tile", None),
        P("member", None, "tile", None),
        P("member", None, "tile", None),
        P("tile", None),
        P(),
    )
    out_specs = (P(None, None, ("member", "tile")), P(None, ("member", "tile")), P())
    return jax.shard_map(local, mesh=mesh, in_specs=in_specs, out_specs=out_specs, check_vma=False)
```

profile of v0, /device:TPU:10, one launch (start us, length us, event | category | flops | bytes accessed | tf_op | source)
XLA Modules:
  0.0 139.2 jit_solution(16982006335386744213)
XLA Ops:
  7.3 1.5 %multiply_reduce_fusion = (f32[4,8,256]{2,1,0:T(8,128)S(1)}, f32[4,16,8,256]{3,2,1,0:T(8,128)S(1)}) fusion(f32[4,16,8,256]{3,2,1,0:T(8,128)} %param.7, f32[256]{0:T(256)S(1)} %multiply_cosine_fusion, f32[4,16,8,256]{3,2,1,0:T(8,128)} %param.5, f32[4,16,8,256]{3,2,1,0:T(8,128)} %param.6), kind=kLoop, calls=%fused_computation.7 | loop fusion | flops 516096 | bytes 2130944 | tf_op jit(solution)/shard_map/tzux,pux->tpx/reduce_sum | solution.py:38
  8.7 4.4 %copy.34 = f32[4,16,8,256]{1,2,0,3:T(8,128)} copy(f32[4,16,8,256]{3,2,1,0:T(8,128)S(1)} %get-tuple-element.16) | data formatting | bytes 1048576 | tf_op jit(solution)/shard_map/mul | solution.py:28
  13.2 9.7 %multiply_bitcast_fusion = f32[4,10,16,256]{2,1,0,3:T(8,128)} fusion(f32[4,16,8,256]{1,2,0,3:T(8,128)} %copy.34, s32[8,256]{0,1:T(8,128)S(1)} %copy.33), kind=kOutput, calls=%fused_computation | convolution fusion | flops 15912960 | bytes 1187840 | tf_op jit(solution)/shard_map/mkxl,bxl->mbkl/dot_general | solution.py:32
  22.9 5.3 %copy.35 = f32[4,10,16,256]{3,2,1,0:T(8,128)S(1)} copy(f32[4,10,16,256]{2,1,0,3:T(8,128)} %multiply_bitcast_fusion) | data formatting | bytes 1310720 | tf_op jit(solution)/shard_map/div | solution.py:32
  28.2 0.2 copy.36
  28.4 1.1 fusion
  29.5 0.2 copy.37
  29.8 0.4 copy.38
  30.2 17.1 %all_to_all.18 = f32[4,170,256]{1,0,2:T(4,128)S(1)} all-to-all(f32[4,170,256]{1,0,2:T(4,128)S(1)} %copy.38), channel_id=1, replica_groups=mesh['member'=4,'tile'=8] {'member'}, dimensions={2} | all-to-all | bytes 1392640 | tf_op jit(solution)/shard_map/all_to_all | solution.py:47
  47.3 0.2 copy.39
  47.5 1.1 copy.40
  48.7 29.1 %reduce-scatter.2.cloned.1.call-done = f32[16,170,8]{1,2,0:T(8,128)} async-done(((f32[16,170,64]{1,2,0:T(8,128)}), f32[16,170,8]{1,2,0:T(8,128)}) %reduce-scatter.2.cloned.1.call-update) | async-done | bytes 87056 | tf_op jit(solution)/shard_map/reduce_scatter | solution.py:48
  77.8 1.2 reshape.33
  79.0 2.3 %copy.41 = f32[16,10,16,8]{3,1,2,0:T(8,128)} copy(f32[16,10,16,8]{2,1,3,0:T(8,128)S(1)} %reshape.33) | data formatting | bytes 163840 | tf_op jit(solution)/shard_map/reshape | solution.py:51
  81.3 1.8 %fusion.11 = f32[16,10,16,8]{3,1,2,0:T(8,128)S(1)} fusion(f32[16,10,16,8]{3,1,2,0:T(8,128)} %copy.41), kind=kOutput, calls=%fused_computation.22 | output fusion | flops 307200 | bytes 163840 | tf_op jit(solution)/shard_map/jit(cumsum)/reduce_window_sum | solution.py:50
  83.1 1.1 copy.42
  84.2 0.2 reduce_sum.28
  84.5 0.7 copy.47
  85.3 0.3 reduce_window_sum.14
  85.6 0.3 fusion.5
  85.9 0.3 convolution_multiply_fusion.1
  86.3 44.7 %psum.7 = f32[16,16,16]{2,0,1:T(8,128)S(1)} all-reduce(f32[16,16,16]{2,0,1:T(8,128)S(1)} %convolution_multiply_fusion.1), channel_id=1, replica_groups=mesh['member'=4,'tile'=8] {'member','tile'}, use_global_device_ids=true, to_apply=%region_5.6 | all-reduce | flops 4096 | bytes 32768 | tf_op jit(solution)/shard_map/psum | solution.py:65
  131.0 0.7 copy.48
  131.8 0.6 broadcast_multiply_fusion.1
  (17 shorter events, 0.7 us)
Async XLA Ops:
  7.2 5.9 %copy-start.1 = (s32[8,256]{1,0:T(8,128)S(1)}, s32[8,256]{1,0:T(8,128)}, u32[]{:S(2)}) copy-start(s32[8,256]{1,0:T(8,128)} %param.8) | copy-start | bytes 24580
  7.2 70.6 %reduce-scatter.2.cloned.1.call-start = ((), (), s32[]{:S(2)}) async-start(), calls=%async_computation.2 | async-start | bytes 1179648 | tf_op jit(solution)/shard_map/reduce_scatter | solution.py:48
  29.8 18.8 %copy-start.2 = (s32[256]{0:T(256)S(1)}, s32[256]{0:T(256)}, u32[]{:S(2)}) copy-start(s32[256]{0:T(256)} %param.9) | copy-start | bytes 3076
  83.1 48.6 %copy-start = (f32[16,170,8]{1,2,0:T(8,128)S(1)}, f32[16,170,8]{1,2,0:T(8,128)}, u32[]{:S(2)}) copy-start(f32[16,170,8]{1,2,0:T(8,128)} %reduce-scatter.2.cloned.1.call-done) | copy-start | bytes 261124
Sparse Core Ops, SparseCore 0:
  48.7 29.0 reduce-scatter.1
where the time goes:
time: 140 us; the launch traced here: 139 us
  blocking collectives  61.8 us (44%)
  waiting for transfers between devices  29.1 us (21%)
  local copies, waits for them, and re-layouts  18.4 us (13%)
  between operations  14.2 us (10%)
  matrix products  11.3 us (8%)
  other arithmetic  4.26 us (3%)
    psum x1, blocking collectives, local(): covariance = lax.psum(local_cov, ('member', 'tile'))  44.7 us
    reduce_scatter x1, waiting for transfers between devices, local(): lax.psum_scatter(regrouped, 'tile', scatter_dimension=2, tiled=True)  29.1 us
    all_to_all x1, blocking collectives, local(): lax.all_to_all(partial_value, 'member', split_axis=2, concat_axis=0, tile...  17.1 us
    dot_general x1, matrix products, local(): jnp.einsum('mkxl,bxl->mbkl', northward_volume_carriage, region_indicator_...  9.66 us
    div x1, local copies, waits for them, and re-layouts, local(): jnp.einsum('mkxl,bxl->mbkl', northward_volume_carriage, region_indicator_...  5.26 us
    mul x1, local copies, waits for them, and re-layouts, local(): northward_speed_field * level_depth_extent * metric_factor(lats)  4.36 us
    reshape x2, local copies, waits for them, and re-layouts, local(): summed[:, :BASINS * layers].reshape(members, BASINS, layers, owned)  3.48 us
  transfers between devices with their start and end apart: 1, of which 1 were waited for; matrix products, arithmetic and copies ran while one was open for 0% of the time, Pallas kernels for 0%

commit v1 on v0

--- a/solution.py
+++ b/solution.py
@@ -62,7 +62,7 @@
     products = jnp.einsum("mfl,nfl->lmn", anomaly, anomaly, precision=greatest_bound_value)
     norm = float((members - 1) * BASINS * layers * (lats // NBANDS))
     local_cov = jnp.einsum("lmn,lc->cmn", products, band_hot, precision=greatest_bound_value) / norm
-    covariance = lax.psum(local_cov, ("member", "tile"))
+    covariance = jnp.sum(lax.all_gather(local_cov, ("member", "tile")), axis=0)
     return (mean_psi, mean_heat, covariance)
 
 

time: 140 us -> 168 us (1.20)
  the two profiles are of different devices: /device:TPU:10 before, /device:TPU:0 now
where the time goes in v1:
time: 168 us
  blocking collectives  84.7 us (50%)
  waiting for transfers between devices  32.4 us (19%)
  local copies, waits for them, and re-layouts  18.4 us (11%)
  between operations  14.2 us (8%)
  matrix products  11.3 us (7%)
  other arithmetic  6.74 us (4%)
    all_gather x1, blocking collectives, local(): covariance = jnp.sum(lax.all_gather(local_cov, ('member', 'tile')), axis=0)  65.5 us
    reduce_scatter x1, waiting for transfers between devices, local(): lax.psum_scatter(regrouped, 'tile', scatter_dimension=2, tiled=True)  32.4 us
    all_to_all x1, blocking collectives, local(): lax.all_to_all(partial_value, 'member', split_axis=2, concat_axis=0, tile...  19.1 us
    dot_general x1, matrix products, local(): jnp.einsum('mkxl,bxl->mbkl', northward_volume_carriage, region_indicator_...  9.66 us
    div x1, local copies, waits for them, and re-layouts, local(): jnp.einsum('mkxl,bxl->mbkl', northward_volume_carriage, region_indicator_...  5.26 us
    mul x1, local copies, waits for them, and re-layouts, local(): northward_speed_field * level_depth_extent * metric_factor(lats)  4.36 us
    reshape x2, local copies, waits for them, and re-layouts, local(): summed[:, :BASINS * layers].reshape(members, BASINS, layers, owned)  3.48 us
  transfers between devices with their start and end apart: 1, of which 1 were waited for; matrix products, arithmetic and copies ran while one was open for 0% of the time, Pallas kernels for 0%

profile of v1, /device:TPU:0, one launch (start us, length us, event | category | flops | bytes accessed | tf_op | source)
XLA Modules:
  0.0 167.8 jit_solution(10977340683092625910)
XLA Ops:
  7.3 1.5 multiply_reduce_fusion
  8.7 4.4 %copy.31 = f32[4,16,8,256]{1,2,0,3:T(8,128)} copy(f32[4,16,8,256]{3,2,1,0:T(8,128)S(1)} %get-tuple-element.7) | data formatting | bytes 1048576 | tf_op jit(solution)/shard_map/mul | solution.py:28
  13.2 9.7 %multiply_bitcast_fusion = f32[4,10,16,256]{2,1,0,3:T(8,128)} fusion(f32[4,16,8,256]{1,2,0,3:T(8,128)} %copy.31, s32[8,256]{0,1:T(8,128)S(1)} %copy.30), kind=kOutput, calls=%fused_computation | convolution fusion | flops 15912960 | bytes 1187840 | tf_op jit(solution)/shard_map/mkxl,bxl->mbkl/dot_general | solution.py:32
  22.9 5.3 %copy.32 = f32[4,10,16,256]{3,2,1,0:T(8,128)S(1)} copy(f32[4,10,16,256]{2,1,0,3:T(8,128)} %multiply_bitcast_fusion) | data formatting | bytes 1310720 | tf_op jit(solution)/shard_map/div | solution.py:32
  28.2 0.2 copy.33
  28.4 1.1 fusion
  29.5 0.2 copy.34
  29.8 0.4 copy.35
  30.2 19.1 %all_to_all.18 = f32[4,170,256]{1,0,2:T(4,128)S(1)} all-to-all(f32[4,170,256]{1,0,2:T(4,128)S(1)} %copy.35), channel_id=1, replica_groups=mesh['member'=4,'tile'=8] {'member'}, dimensions={2} | all-to-all | bytes 1392640 | tf_op jit(solution)/shard_map/all_to_all | solution.py:47
  49.3 0.2 copy.36
  49.5 1.1 copy.37
  50.7 32.4 %reduce-scatter.2.cloned.1.call-done = f32[16,170,8]{1,2,0:T(8,128)} async-done(((f32[16,170,64]{1,2,0:T(8,128)}), f32[16,170,8]{1,2,0:T(8,128)}) %reduce-scatter.2.cloned.1.call-update) | async-done | bytes 87056 | tf_op jit(solution)/shard_map/reduce_scatter | solution.py:48
  83.1 1.2 reshape.33
  84.3 2.3 %copy.38 = f32[16,10,16,8]{3,1,2,0:T(8,128)} copy(f32[16,10,16,8]{2,1,3,0:T(8,128)S(1)} %reshape.33) | data formatting | bytes 163840 | tf_op jit(solution)/shard_map/reshape | solution.py:51
  86.6 1.8 %fusion.11 = f32[16,10,16,8]{3,1,2,0:T(8,128)S(1)} fusion(f32[16,10,16,8]{3,1,2,0:T(8,128)} %copy.38), kind=kOutput, calls=%fused_computation.22 | output fusion | flops 307200 | bytes 163840 | tf_op jit(solution)/shard_map/jit(cumsum)/reduce_window_sum | solution.py:50
  88.4 1.1 copy.39
  89.8 0.7 copy.44
  90.6 0.3 reduce_window_sum.14
  90.9 0.3 fusion.5
  91.2 0.3 convolution_multiply_fusion.1
  91.5 65.5 %all-gather = f32[512,16,16]{2,0,1:T(8,128)} all-gather(f32[16,16,16]{2,0,1:T(8,128)S(1)} %convolution_multiply_fusion.1), channel_id=2, replica_groups=mesh['member'=4,'tile'=8] {'member','tile'}, dimensions={0}, use_global_device_ids=true | all-gather | bytes 540672 | tf_op jit(solution)/shard_map/all_gather | solution.py:65
  157.1 2.5 %reduce_sum.39 = f32[16,16,16]{2,0,1:T(8,128)S(1)} reduce(f32[32,16,16,16]{3,1,0,2:T(8,128)} %bitcast.28, f32[]{:T(128)} %constant.13.clone.1), dimensions={0}, to_apply=%region_5.6 | reduce | flops 126976 | bytes 540676 | tf_op jit(solution)/shard_map/reduce_sum | solution.py:65
  159.6 0.7 copy.45
  160.3 0.6 broadcast_multiply_fusion.1
  (18 shorter events, 0.9 us)
Async XLA Ops:
  7.2 5.9 %copy-start.1 = (s32[8,256]{1,0:T(8,128)S(1)}, s32[8,256]{1,0:T(8,128)}, u32[]{:S(2)}) copy-start(s32[8,256]{1,0:T(8,128)} %param.8) | copy-start | bytes 24580
  7.2 75.9 %reduce-scatter.2.cloned.1.call-start = ((), (), s32[]{:S(2)}) async-start(), calls=%async_computation.2 | async-start | bytes 1179648 | tf_op jit(solution)/shard_map/reduce_scatter | solution.py:48
  29.8 20.9 %copy-start.2 = (s32[256]{0:T(256)S(1)}, s32[256]{0:T(256)}, u32[]{:S(2)}) copy-start(s32[256]{0:T(256)} %param.9) | copy-start | bytes 3076
  91.5 68.7 %copy-start = (f32[16,170,8]{1,2,0:T(8,128)S(1)}, f32[16,170,8]{1,2,0:T(8,128)}, u32[]{:S(2)}) copy-start(f32[16,170,8]{1,2,0:T(8,128)} %reduce-scatter.2.cloned.1.call-done) | copy-start | bytes 261124
Sparse Core Ops, SparseCore 0:
  50.7 32.3 reduce-scatter.1
